TPU v7x, 32 devices: a whole 2x2x4 slice. The times are simulated.
32 devices in a mesh: mesh: 8 (over z, y), member: 4 (over x, core).
Axes of the slice: x: 2, y: 2, z: 4, core: 2. Of those that a mesh axis runs over, the one named last changes fastest.
Arguments:
- node_states: bfloat16 [8, 4096, 512], P('member', 'mesh'), may hold values from -60 to 60
- projection: bfloat16 [512, 1536], P('member'), may hold values from -12 to 12
- output_weight: bfloat16 [512, 512], P('member'), may hold values from -0.25 to 0.25
- up_weight: bfloat16 [512, 2048], P('member'), may hold values from -0.25 to 0.25
- down_weight: bfloat16 [2048, 512], P('member'), may hold values from -0.125 to 0.125
- attention_gain: float32 [512], replicated, may hold values from 0.5 to 2
- feedforward_gain: float32 [512], replicated, may hold values from 0.5 to 2
- tile_lists: int32 [32, 8], P('mesh'), may hold values from 0 to 31, as said below
- tile_counts: int32 [32], P('mesh'), may hold values from 4 to 8, as said below
Outputs:
- updated_states: bfloat16 [8, 4096, 512], P('member', 'mesh')
Inputs may be any that keep to these rules, and one draw needn't show every extreme that they name: `tile_lists`: entry 0 of tile t's list is t. Every entry names a tile of the device that holds t, or one of the last 4 tiles of the device before it, or one of the first 4 tiles of the device after it along mesh (the first and last devices are neighbours). The first tile_counts[t] entries are distinct; later entries are ignored. `tile_counts`: every device holds a tile whose count is 8.
All inputs are finite; a program needn't handle non-finite values.
Results may differ from a plain program's by a relative error of at most 0.0056.
Values may be sent and summed in bfloat16 or wider, within the bound.
A program may use at most 128 MiB of HBM per device.

v0:
```python
import functools
import math

import jax
import jax.numpy as jnp
from jax import lax
from jax.experimental import pallas as pl
from jax.experimental.pallas import tpu as pltpu
from jax.sharding import PartitionSpec as P

HEADS = 4
RIM_T = 4
MESH = pl.DeviceIdType.MESH
MASKED = -1e30
SHARED = -1
EPS = 1e-05


def norm_rows(rows, gain):
    values = rows.astype(jnp.float32)
    center = values - jnp.mean(values, axis=-1, keepdims=True)
    spread = jnp.mean(center * center, axis=-1, keepdims=True)
    return (center * lax.rsqrt(spread + EPS) * gain).astype(jnp.bfloat16)


def gelu(value):
    inner = math.sqrt(2.0 / math.pi) * (value + 0.044715 * value * value * value)
    return 0.5 * value * (1.0 + jnp.tanh(inner))


def dot(a, b):
    return jnp.dot(a, b, preferred_element_type=jnp.float32)


def kernel(
    ring, party, tiles,
    x_hbm, proj_hbm, wo_hbm, up_hbm, down_hbm, gain1_hbm, gain2_hbm, lists_hbm, counts_hbm,
    out_ref,
    xs, wproj, wo, up, down, q_s, k_s, v_s, acc, top, att, hid, mid, bias, gain1, gain2, lists, counts, out_s,
    local_sem, xp_send, xp_recv, xf_send, xf_recv, w_send, w_recv,
):
    members, rows, width = x_hbm.shape
    tile = rows // tiles
    head = width // HEADS
    groups = party // 2
    me = lax.axis_index("mesh")
    mine = lax.axis_index("member")
    parity = lax.rem(me, 2)
    side = 1 - 2 * parity
    partner = me + side
    onward = lax.rem(me + 2 * side + ring, ring)
    behind = lax.rem(me - 2 * side + ring, ring)
    core = lax.rem(mine, 2)
    twin = mine + 1 - 2 * core
    across = [lax.rem(mine + 2 * d, party) for d in range(1, groups)]

    barrier = pltpu.get_barrier_semaphore()
    for peer in (partner, onward, behind):
        pl.semaphore_signal(barrier, inc=1, device_id={"mesh": peer}, device_id_type=MESH)
    for peer in [twin] + across:
        pl.semaphore_signal(barrier, inc=1, device_id={"member": peer}, device_id_type=MESH)
    pl.semaphore_wait(barrier, 4 + len(across))

    pieces = [(m, t) for m in range(members) for t in range(tiles)]

    def piece(ref, m, t):
        return ref.at[m, pl.ds(t * tile, tile)]

    to_partner = []
    for i, (m, t) in enumerate(pieces):
        to_partner.append(pltpu.make_async_remote_copy(
            src_ref=piece(x_hbm, m, t), dst_ref=piece(xs.at[1], m, t),
            send_sem=xp_send.at[i], recv_sem=xp_recv.at[i],
            device_id={"mesh": partner}, device_id_type=MESH))
    to_onward = []
    for i, (m, t) in enumerate(pieces):
        to_onward.append(pltpu.make_async_remote_copy(
            src_ref=piece(xs.at[1], m, t), dst_ref=piece(xs.at[2], m, t),
            send_sem=xf_send.at[i], recv_sem=xf_recv.at[i],
            device_id={"mesh": onward}, device_id_type=MESH))

    odd = lax.rem(me // 2, 2)
    aside = me + 2 - 4 * odd
    shards = (proj_hbm, wo_hbm, up_hbm, down_hbm)
    wholes = (wproj, wo, up, down)

    def part(w, who):
        depth = shards[w].shape[0]
        return wholes[w].at[pl.ds(pl.multiple_of(who * depth, depth), depth)]

    lanes = 1 + 4 * (groups - 1)

    def weight_copy(w, lane, src, dst, target):
        return pltpu.make_async_remote_copy(
            src_ref=src, dst_ref=dst,
            send_sem=w_send.at[w * lanes + lane], recv_sem=w_recv.at[w * lanes + lane],
            device_id=target, device_id_type=MESH)

    to_twin, to_across, to_side, near_pass, far_pass = [], [], [], [], []
    for w in range(4):
        to_twin.append(weight_copy(w, 0, shards[w], part(w, mine), {"member": twin}))
        for row in (to_across, to_side, near_pass, far_pass):
            row.append([])
        depth = shards[w].shape[0] // 2

        def half_part(who, which):
            return wholes[w].at[pl.ds(pl.multiple_of((2 * who + which) * depth, depth), depth)]

        for d in range(1, groups):
            giver = lax.rem(mine + party - 2 * d, party)
            lane = 4 * d - 3
            if w == SHARED:
                got, other = half_part(giver, odd), half_part(giver, 1 - odd)
                to_across[w].append(weight_copy(
                    w, lane, shards[w].at[pl.ds(pl.multiple_of(odd * depth, depth), depth)],
                    half_part(mine, odd), {"member": across[d - 1]}))
                to_side[w].append(weight_copy(w, lane + 2, got, got, {"mesh": aside}))
                far_pass[w].append(weight_copy(w, lane + 3, other, other, {"member": twin}))
            else:
                got = part(w, giver)
                to_across[w].append(weight_copy(
                    w, lane, shards[w], part(w, mine), {"member": across[d - 1]}))
            near_pass[w].append(weight_copy(w, lane + 1, got, got, {"member": twin}))

    for copy in to_across[0]:
        copy.start()
    to_partner[0].start()
    to_twin[0].start()
    for copy in to_partner[1:]:
        copy.start()
    for w in range(1, 4):
        for copy in to_across[w]:
            copy.start()
        to_twin[w].start()
    x_local = pltpu.make_async_copy(x_hbm, xs.at[0], local_sem.at[0])
    x_local.start()
    w_local = [pltpu.make_async_copy(shards[w], part(w, mine), local_sem.at[1 + w])
               for w in range(4)]
    for copy in w_local:
        copy.start()
    small = [pltpu.make_async_copy(src, dst, local_sem.at[5 + i]) for i, (src, dst) in enumerate(
        ((gain1_hbm, gain1), (gain2_hbm, gain2), (lists_hbm, lists), (counts_hbm, counts)))]
    for copy in small:
        copy.start()
    v_s[:, :, head:] = jnp.ones((HEADS, rows, head), jnp.bfloat16)
    for copy in small:
        copy.wait()

    def pass_near(w):
        for d in range(groups - 1):
            to_across[w][d].wait_recv()
            if w == SHARED:
                to_side[w][d].start()
            near_pass[w][d].start()

    def pass_far(w):
        for d in range(groups - 1):
            to_side[w][d].wait_recv()
            far_pass[w][d].start()

    def have_weight(w):
        w_local[w].wait()
        to_twin[w].wait_recv()
        for copy in near_pass[w] + far_pass[w]:
            copy.wait_recv()

    def pass_pieces(first, last):
        for i in range(first, last):
            to_partner[i].wait_recv()
            to_onward[i].start()

    every = tiles * ring
    start = me * tiles

    def fill_bias(t, carry):
        count = counts[t]
        places = []
        for j in range(lists.shape[1]):
            place = lists[t, j] - start + RIM_T
            place = jnp.where(place < 0, place + every, place)
            place = jnp.where(place >= every, place - every, place)
            places.append(jnp.where(j < count, place, -1))
        for c in range(3 * tiles):
            if c < tiles:
                want = RIM_T + c
            elif c < 2 * tiles:
                want = jnp.where(parity == 0, RIM_T + tiles + c - tiles, RIM_T - tiles + c - tiles)
            else:
                want = jnp.where(parity == 0, RIM_T - tiles + c - 2 * tiles, RIM_T + tiles + c - 2 * tiles)
            hit = places[0] == want
            for place in places[1:]:
                hit = jnp.logical_or(hit, place == want)
            bias[t, c] = jnp.where(hit, 0.0, MASKED)
        return carry

    lax.fori_loop(0, tiles, fill_bias, 0)

    query_scale = math.log2(math.e) / math.sqrt(head)

    def project(slot, m):
        normed = norm_rows(xs[slot, m], gain1[...].reshape(1, width))
        if slot == 0:
            queries = (dot(normed, wproj[:, :width]) * query_scale).astype(jnp.bfloat16)
            for h in range(HEADS):
                q_s[m, h] = queries[:, h * head:(h + 1) * head]
        keys = dot(normed, wproj[:, width:2 * width]).astype(jnp.bfloat16)
        for h in range(HEADS):
            k_s[h] = keys[:, h * head:(h + 1) * head]
        values = dot(normed, wproj[:, 2 * width:]).astype(jnp.bfloat16)
        for h in range(HEADS):
            v_s[h, :, :head] = values[:, h * head:(h + 1) * head]

    together = 2

    def attend(slot, m):
        marks = [[bias[t, slot * tiles + c] for c in range(tiles)] for t in range(tiles)]

        def body(pair, carry):
            for i in range(together):
                h = pair * together + i
                scores = lax.dot_general(
                    q_s[m, h], k_s[h], (((1,), (1,)), ((), ())),
                    preferred_element_type=jnp.float32)
                packed, fades = [], []
                for t in range(tiles):
                    here = slice(t * tile, (t + 1) * tile)
                    parts = [scores[here, c * tile:(c + 1) * tile] + marks[t][c]
                             for c in range(tiles)]
                    best = parts[0]
                    for p in parts[1:]:
                        best = jnp.maximum(best, p)
                    best = jnp.broadcast_to(jnp.max(best, axis=-1, keepdims=True), (tile, tile))
                    if slot > 0:
                        old = top[m, h, here, :]
                        best = jnp.maximum(best, old)
                        fades.append(jnp.exp2(old - best))
                    if slot < 2:
                        top[m, h, here, :] = best
                    packed.append(jnp.concatenate(
                        [jnp.exp2(p - best).astype(jnp.bfloat16) for p in parts], axis=1))
                blended = dot(jnp.concatenate(packed, axis=0), v_s[h])
                if slot > 0:
                    fade = jnp.concatenate(fades, axis=0)
                    blended = blended + acc[m, h] * jnp.concatenate([fade, fade], axis=1)
                if slot < 2:
                    acc[m, h] = blended
                else:
                    att[h, m] = (blended[:, :head] / blended[:, head:]).astype(jnp.bfloat16)
            return carry

        lax.fori_loop(0, HEADS // together, body, 0)

    inner = up.shape[1]
    cut = width

    def expand(m):
        blended = jnp.concatenate([att[h, m] for h in range(HEADS)], axis=1)
        middle = (xs[0, m].astype(jnp.float32) + dot(blended, wo[...])).astype(jnp.bfloat16)
        mid[m] = middle
        normed = norm_rows(middle, gain2[...].reshape(1, width))
        for c in range(inner // cut):
            hid[m, :, c * cut:(c + 1) * cut] = gelu(
                dot(normed, up[:, c * cut:(c + 1) * cut])).astype(jnp.bfloat16)

    def finish(m):
        out_s[m] = (mid[m].astype(jnp.float32) + dot(hid[m], down[...])).astype(jnp.bfloat16)

    count = len(pieces)
    late = count // 2
    def far_here(m):
        for t in range(tiles):
            to_onward[m * tiles + t].wait_recv()

    pass_near(0)
    pass_pieces(0, 1)

    have_weight(0)
    x_local.wait()
    project(0, 0)
    pass_pieces(1, 2)
    attend(0, 0)
    pass_near(1)
    project(0, 1)
    pass_pieces(2, late - 1)
    attend(0, 1)
    pass_pieces(late - 1, late)
    project(1, 0)
    attend(1, 0)
    pass_pieces(late, late + 1)
    far_here(0)
    project(2, 0)
    pass_pieces(late + 1, late + 2)
    pass_near(2)
    attend(2, 0)
    pass_pieces(late + 2, late + 3)
    have_weight(1)
    have_weight(2)
    expand(0)
    pass_pieces(late + 3, count)
    project(1, 1)
    attend(1, 1)
    far_here(1)
    project(2, 1)
    attend(2, 1)
    pass_near(3)
    expand(1)
    have_weight(3)
    stores = []
    for m in range(members):
        finish(m)
        stores.append(pltpu.make_async_copy(out_s.at[m], out_ref.at[m], local_sem.at[9 + m]))
        stores[m].start()
    for copy in stores:
        copy.wait()
    for copy in to_partner + to_onward + to_twin:
        copy.wait_send()
    for w in range(4):
        for copy in to_across[w] + to_side[w] + near_pass[w] + far_pass[w]:
            copy.wait_send()


def solution(mesh):
    ring, party = mesh.shape["mesh"], mesh.shape["member"]

    def on_device(node_states, projection, output_weight, up_weight, down_weight,
                  attention_gain, feedforward_gain, tile_lists, tile_counts):
        members, rows, width = node_states.shape
        tiles = tile_lists.shape[0]
        head = width // HEADS
        inner = up_weight.shape[1]
        hbm = pl.BlockSpec(memory_space=pltpu.HBM)
        bf16, f32 = jnp.bfloat16, jnp.float32
        copies = members * tiles
        lanes = 1 + 4 * (party // 2 - 1)
        return pl.pallas_call(
            functools.partial(kernel, ring, party, tiles),
            out_shape=jax.ShapeDtypeStruct(node_states.shape, bf16),
            in_specs=[hbm] * 9,
            out_specs=hbm,
            scratch_shapes=[
                pltpu.VMEM((3, members, rows, width), bf16),
                pltpu.VMEM((width, 3 * width), bf16),
                pltpu.VMEM((width, width), bf16),
                pltpu.VMEM((width, inner), bf16),
                pltpu.VMEM((inner, width), bf16),
                pltpu.VMEM((members, HEADS, rows, head), bf16),
                pltpu.VMEM((HEADS, rows, head), bf16),
                pltpu.VMEM((HEADS, rows, 2 * head), bf16),
                pltpu.VMEM((members, HEADS, rows, 2 * head), f32),
                pltpu.VMEM((members, HEADS, rows, head), f32),
                pltpu.VMEM((HEADS, members, rows, head), bf16),
                pltpu.VMEM((members, rows, inner), bf16),
                pltpu.VMEM((members, rows, width), bf16),
                pltpu.SMEM((tiles, 3 * tiles), f32),
                pltpu.VMEM((width,), f32),
                pltpu.VMEM((width,), f32),
                pltpu.SMEM(tile_lists.shape, jnp.int32),
                pltpu.SMEM(tile_counts.shape, jnp.int32),
                pltpu.VMEM((members, rows, width), bf16),
                pltpu.SemaphoreType.DMA((9 + members,)),
                pltpu.SemaphoreType.DMA((copies,)),
                pltpu.SemaphoreType.DMA((copies,)),
                pltpu.SemaphoreType.DMA((copies,)),
                pltpu.SemaphoreType.DMA((copies,)),
                pltpu.SemaphoreType.DMA((4 * lanes,)),
                pltpu.SemaphoreType.DMA((4 * lanes,)),
            ],
            compiler_params=pltpu.CompilerParams(
                collective_id=0, has_side_effects=True, vmem_limit_bytes=67043328
            ),
        )(node_states, projection, output_weight, up_weight, down_weight,
          attention_gain, feedforward_gain, tile_lists, tile_counts)

    in_specs = (
        P("member", "mesh", None), P("member", None), P("member", None),
        P("member", None), P("member", None), P(), P(), P("mesh", None), P("mesh"),
    )
    return jax.shard_map(
        on_device, mesh=mesh, in_specs=in_specs,
        out_specs=P("member", "mesh", None), check_vma=False)
```

profile of v0, /device:TPU:0, one launch (start us, length us, event | category | flops | bytes accessed | tf_op | source)
XLA Modules:
  0.0 53.5 jit_solution(11358376894385963263)
XLA Ops:
  0.0 51.2 %shard_map.91 = bf16[2,512,512]{2,1,0:T(8,128)(2,1)} custom-call(bf16[2,512,512]{2,1,0:T(8,128)(2,1)} %x_hbm.1, bf16[128,1536]{1,0:T(8,128)(2,1)} %proj_hbm.1, bf16[128,512]{1,0:T(8,128)(2,1)} %wo_hbm.1, bf16[128,2048]{1,0:T(8,128)(2,1)} %up_hbm.1, bf16[512,512]{1,0:T(8,128)(2,1)} %down_hbm.1, f32[512]{0:T(512)} %gain1_hbm.1, f32[512]{0:T(512)} %gain2_hbm.1, ...), custom_call_target="tpu_custom_call" | custom-call | tf_op jit(solution)/shard_map/pallas_call | solution.py:335
  51.2 2.3 %copy.11 = bf16[2,512,512]{2,1,0:T(8,128)(2,1)} copy(bf16[2,512,512]{2,1,0:T(8,128)(2,1)} %shard_map.91) | data formatting | bytes 2097152
where the time goes:
time: 53.7 us; the launch traced here: 53.5 us
  Pallas kernels  51.2 us (95%)
  local copies, waits for them, and re-layouts  2.26 us (4%)
    pallas_call x1, Pallas kernels, on_device(): pl.pallas_call(functools.partial(kernel, ring, party, tiles), out_shape=j...  51.2 us
    unnamed x1, local copies, waits for them, and re-layouts  2.26 us

commit v1 on v0

--- a/solution.py
+++ b/solution.py
@@ -36,7 +36,7 @@
     ring, party, tiles,
     x_hbm, proj_hbm, wo_hbm, up_hbm, down_hbm, gain1_hbm, gain2_hbm, lists_hbm, counts_hbm,
     out_ref,
-    xs, wproj, wo, up, down, q_s, k_s, v_s, acc, top, att, hid, mid, bias, gain1, gain2, lists, counts, out_s,
+    xs, wproj, wo, up, down, q_s, k_s, v_s, acc, top, att, hid, mid, bias, gain1, gain2, lists, counts,
     local_sem, xp_send, xp_recv, xf_send, xf_recv, w_send, w_recv,
 ):
     members, rows, width = x_hbm.shape
@@ -263,7 +263,7 @@
                 dot(normed, up[:, c * cut:(c + 1) * cut])).astype(jnp.bfloat16)
 
     def finish(m):
-        out_s[m] = (mid[m].astype(jnp.float32) + dot(hid[m], down[...])).astype(jnp.bfloat16)
+        out_ref[m] = (mid[m].astype(jnp.float32) + dot(hid[m], down[...])).astype(jnp.bfloat16)
 
     count = len(pieces)
     late = count // 2
@@ -308,8 +308,6 @@
     stores = []
     for m in range(members):
         finish(m)
-        stores.append(pltpu.make_async_copy(out_s.at[m], out_ref.at[m], local_sem.at[9 + m]))
-        stores[m].start()
     for copy in stores:
         copy.wait()
     for copy in to_partner + to_onward + to_twin:
@@ -334,9 +332,9 @@
         lanes = 1 + 4 * (party // 2 - 1)
         return pl.pallas_call(
             functools.partial(kernel, ring, party, tiles),
-            out_shape=jax.ShapeDtypeStruct(node_states.shape, bf16),
+            out_shape=pltpu.VMEM(node_states.shape, bf16),
             in_specs=[hbm] * 9,
-            out_specs=hbm,
+            out_specs=pl.BlockSpec(memory_space=pltpu.VMEM),
             scratch_shapes=[
                 pltpu.VMEM((3, members, rows, width), bf16),
                 pltpu.VMEM((width, 3 * width), bf16),
@@ -356,7 +354,6 @@
                 pltpu.VMEM((width,), f32),
                 pltpu.SMEM(tile_lists.shape, jnp.int32),
                 pltpu.SMEM(tile_counts.shape, jnp.int32),
-                pltpu.VMEM((members, rows, width), bf16),
                 pltpu.SemaphoreType.DMA((9 + members,)),
                 pltpu.SemaphoreType.DMA((copies,)),
                 pltpu.SemaphoreType.DMA((copies,)),
@@ -366,7 +363,7 @@
                 pltpu.SemaphoreType.DMA((4 * lanes,)),
             ],
             compiler_params=pltpu.CompilerParams(
-                collective_id=0, has_side_effects=True, vmem_limit_bytes=67043328
+                collective_id=0, has_side_effects=True, vmem_limit_bytes=60000000
             ),
         )(node_states, projection, output_weight, up_weight, down_weight,
           attention_gain, feedforward_gain, tile_lists, tile_counts)

time: 53.7 us -> 51.5 us (0.959)
  local copies, waits for them, and re-layouts: 2.26 us -> 0.97 us
  Pallas kernels: 51.2 us -> 50.4 us
    unnamed x1, local copies, waits for them, and re-layouts: 2.26 us -> 0.97 us
    pallas_call x1, Pallas kernels: 51.2 us -> 50.4 us  [on_device(): pl.pallas_call(functools.partial(kernel, ring, party, tiles), out_shape=p...]
where the time goes in v1:
time: 51.5 us; the launch traced here: 51.4 us
  Pallas kernels  50.4 us (98%)
  local copies, waits for them, and re-layouts  0.97 us (2%)
    pallas_call x1, Pallas kernels, on_device(): pl.pallas_call(functools.partial(kernel, ring, party, tiles), out_shape=p...  50.4 us

profile of v1, /device:TPU:0, one launch (start us, length us, event | category | flops | bytes accessed | tf_op | source)
XLA Modules:
  0.0 51.4 jit_solution(7587186673677444787)
XLA Ops:
  0.0 50.4 %shard_map.91 = bf16[2,512,512]{2,1,0:T(8,128)(2,1)S(1)} custom-call(bf16[2,512,512]{2,1,0:T(8,128)(2,1)} %x_hbm.1, bf16[128,1536]{1,0:T(8,128)(2,1)} %proj_hbm.1, bf16[128,512]{1,0:T(8,128)(2,1)} %wo_hbm.1, bf16[128,2048]{1,0:T(8,128)(2,1)} %up_hbm.1, bf16[512,512]{1,0:T(8,128)(2,1)} %down_hbm.1, f32[512]{0:T(512)} %gain1_hbm.1, f32[512]{0:T(512)} %gain2_hbm.1, ...), custom_call_target="tpu_custom_call" | custom-call | tf_op jit(solution)/shard_map/pallas_call | solution.py:333
  50.4 1.0 %copy.11 = bf16[2,512,512]{2,1,0:T(8,128)(2,1)} copy(bf16[2,512,512]{2,1,0:T(8,128)(2,1)S(1)} %shard_map.91) | data formatting | bytes 2097152

commit v2 on v1

v2 whole, which is shorter than its diff:
```python
import functools
import math

import jax
import jax.numpy as jnp
from jax import lax
from jax.experimental import pallas as pl
from jax.experimental.pallas import tpu as pltpu
from jax.sharding import PartitionSpec as P

HEADS = 4
RIM_T = 4
MESH = pl.DeviceIdType.MESH
MASKED = -1e30
EPS = 1e-05
SLOTS = 42
PROJ_VIA = (None, None, None, None)
UP_CUTS = 2
DOWN_SHARED = 12
DOWN_CUTS = 3
PIECES = 2
CUT = 256
ORDER = [[(0, 0), (0, 1), (0, 2), (0, 3), (1, 0), (1, 1), (1, 2), (1, 3), (2, 0), (2, 1), (2, 2), (2, 3)], [(0, 0), (0, 1), (0, 2), (0, 3), (1, 0), (1, 1), (1, 2), (2, 0), (2, 1), (1, 3), (2, 2), (2, 3)]]


def norm_rows(rows, gain):
    values = rows.astype(jnp.float32)
    center = values - jnp.mean(values, axis=-1, keepdims=True)
    spread = jnp.mean(center * center, axis=-1, keepdims=True)
    return (center * lax.rsqrt(spread + EPS) * gain).astype(jnp.bfloat16)


def gelu(value):
    inner = math.sqrt(2.0 / math.pi) * (value + 0.044715 * value * value * value)
    return 0.5 * value * (1.0 + jnp.tanh(inner))


def dot(a, b):
    return jnp.dot(a, b, preferred_element_type=jnp.float32)


def kernel(
    ring, party, tiles,
    x_hbm, proj_hbm, wo_hbm, up_hbm, down_hbm, gain1_hbm, gain2_hbm, lists_hbm, counts_hbm,
    out_ref,
    xs, xn, wproj, wo, up, down, q_s, k_s, v_s, acc, top, att, hid, mid, nrm, bias,
    gain1, gain2, lists, counts,
    local_sem, xp_send, xp_recv, xf_send, xf_recv, w_send, w_recv,
):
    members, rows, width = x_hbm.shape
    tile = rows // tiles
    head = width // HEADS
    groups = party // 2
    inner = up.shape[1]
    me = lax.axis_index("mesh")
    mine = lax.axis_index("member")
    parity = lax.rem(me, 2)
    side = 1 - 2 * parity
    partner = me + side
    onward = lax.rem(me + 2 * side + ring, ring)
    behind = lax.rem(me - 2 * side + ring, ring)
    core = lax.rem(mine, 2)
    twin = mine + 1 - 2 * core
    across = [lax.rem(mine + 2 * d, party) for d in range(1, groups)]

    w_local = []

    def part(ref, who, depth, start, size):
        return ref.at[pl.ds(pl.multiple_of(who * depth + start, 16), size)]

    small = [pltpu.make_async_copy(src, dst, local_sem.at[i]) for i, (src, dst) in enumerate(
        ((lists_hbm, lists), (counts_hbm, counts), (gain1_hbm, gain1), (gain2_hbm, gain2)))]
    for copy in small:
        copy.start()
    x_local = pltpu.make_async_copy(x_hbm, xs.at[0], local_sem.at[4])
    x_local.start()

    barrier = pltpu.get_barrier_semaphore()
    for peer in (partner, onward, behind):
        pl.semaphore_signal(barrier, inc=1, device_id={"mesh": peer}, device_id_type=MESH)
    for peer in [twin] + across:
        pl.semaphore_signal(barrier, inc=1, device_id={"member": peer}, device_id_type=MESH)

    local_count = [5]

    def local(src, dst):
        copy = pltpu.make_async_copy(src, dst, local_sem.at[local_count[0]])
        local_count[0] += 1
        copy.start()
        return copy

    def head_blocks(h, who, start, size):
        depth = proj_hbm.shape[0]
        return [(proj_hbm.at[pl.ds(start, size), pl.ds(j * width + h * head, head)],
                 wproj.at[h, pl.ds(pl.multiple_of(who * depth + start, 16), size),
                          pl.ds(j * head, head)]) for j in range(3)]

    def row_blocks(shard, whole, who, start, size):
        return [(shard.at[pl.ds(start, size)], part(whole, who, shard.shape[0], start, size))]

    def blocks_of(unit, who, start, size):
        kind, h = unit
        if kind == "proj":
            return head_blocks(h, who, start, size)
        shard, whole = {"wo": (wo_hbm, wo), "up": (up_hbm, up), "down": (down_hbm, down)}[kind]
        return row_blocks(shard, whole, who, start, size)

    proj_local = []
    for h in range(HEADS):
        for s, d in head_blocks(h, mine, 0, proj_hbm.shape[0]):
            pltpu.make_async_copy(s, d, local_sem.at[8 + h]).start()
        whole = wproj.at[h, pl.ds(0, proj_hbm.shape[0])]
        proj_local.append([pltpu.make_async_copy(whole, whole, local_sem.at[8 + h])])
    rest_local = {name: local(shard, part(whole, mine, shard.shape[0], 0, shard.shape[0]))
                  for name, shard, whole in
                  (("wo", wo_hbm, wo), ("up", up_hbm, up), ("down", down_hbm, down))}

    used = [0]
    moved = [0] * 5

    odd = lax.rem(me // 2, 2)
    beside = me + 2 - 4 * odd

    class Stream:
        def __init__(self, way, pairs, target):
            self.pairs, self.way = pairs, way
            self.index = used[0]
            used[0] += 1
            self.size = sum(math.prod(s.shape) for s, _ in pairs) // width
            moved[way] += self.size
            self.target = target

        def copy(self, src, dst):
            return pltpu.make_async_remote_copy(
                src_ref=src, dst_ref=dst, send_sem=w_send.at[self.way],
                recv_sem=w_recv.at[self.index], device_id=self.target, device_id_type=MESH)

        def start(self):
            for s, d in self.pairs:
                self.copy(s, d).start()

        def wait_recv(self):
            whole = down.at[pl.ds(0, self.size)]
            self.copy(whole, whole).wait_recv()

    class Unit:
        def __init__(self, name, start, size, via=None):
            over_pairs, near_pairs, mate_pairs, far_pairs = [], [], [], []
            self.twin = [Stream(0, blocks_of(name, mine, start, size), {"member": twin})]
            self.over, self.near, self.mate, self.far = [], [], [], []
            for d in range(1, groups):
                giver = lax.rem(mine + party - 2 * d, party)
                if via is None:
                    got, part_size = start, size
                else:
                    pick, mate = (odd, beside) if via == "z" else (parity, partner)
                    part_size = size // 2
                    got = pl.multiple_of(start + pick * part_size, 16)
                    other = pl.multiple_of(start + (1 - pick) * part_size, 16)
                self.over.append(Stream(1, blocks_of(name, mine, got, part_size),
                                        {"member": across[d - 1]}))
                here = [(t, t) for _, t in blocks_of(name, giver, got, part_size)]
                self.near.append(Stream(2, here, {"member": twin}))
                if via is not None:
                    self.mate.append(Stream(3, here, {"mesh": mate}))
                    self.far.append(Stream(
                        4, [(t, t) for _, t in blocks_of(name, giver, other, part_size)],
                        {"member": twin}))

        def send_twin(self):
            for stream in self.twin:
                stream.start()

        def send_over(self):
            for stream in self.over:
                stream.start()

        def pass_near(self):
            for stream in self.over:
                stream.wait_recv()
            for stream in self.mate + self.near:
                stream.start()

        def pass_far(self):
            for stream in self.mate:
                stream.wait_recv()
            for stream in self.far:
                stream.start()

        def have(self):
            for stream in self.twin + self.near + self.far:
                stream.wait_recv()

    deep = proj_hbm.shape[0]
    proj_units = [Unit(("proj", h), 0, deep, PROJ_VIA[h]) for h in range(HEADS)]
    wo_units = [Unit(("wo", 0), 0, wo_hbm.shape[0])]
    up_depth = up_hbm.shape[0]
    up_units = [Unit(("up", 0), i * up_depth // UP_CUTS, up_depth // UP_CUTS)
                for i in range(UP_CUTS)]
    down_depth = down_hbm.shape[0]
    shared = down_depth * DOWN_SHARED // 16
    down_shared = [Unit(("down", 0), i * shared // DOWN_CUTS, shared // DOWN_CUTS, "y")
                   for i in range(DOWN_CUTS)] if shared else []
    down_direct = [Unit(("down", 0), shared + i * (down_depth - shared) // 2,
                        (down_depth - shared) // 2) for i in range(2)]
    down_units = down_shared + down_direct
    all_units = proj_units + wo_units + up_units + down_units

    piece = tile // PIECES
    steps = [(m, i * piece) for m in range(members) for i in range(rows // piece)]
    to_partner, to_onward = [], []
    for i, (m, start) in enumerate(steps):
        to_partner.append(pltpu.make_async_remote_copy(
            src_ref=x_hbm.at[m, pl.ds(start, piece)], dst_ref=xs.at[1, m, pl.ds(start, piece)],
            send_sem=xp_send, recv_sem=xp_recv.at[i],
            device_id={"mesh": partner}, device_id_type=MESH))
        to_onward.append(pltpu.make_async_remote_copy(
            src_ref=xs.at[1, m, pl.ds(start, piece)], dst_ref=xs.at[2, m, pl.ds(start, piece)],
            send_sem=xf_send, recv_sem=xf_recv.at[i],
            device_id={"mesh": onward}, device_id_type=MESH))

    pl.semaphore_wait(barrier, 4 + len(across))

    proj_units[0].send_over()
    to_partner[0].start()
    proj_units[0].send_twin()
    for copy in to_partner[1:]:
        copy.start()
    for unit in proj_units[1:]:
        unit.send_over()
        unit.send_twin()
    for unit in wo_units + up_units + down_units:
        unit.send_over()
    for unit in wo_units + up_units + down_units:
        unit.send_twin()

    for m in range(members):
        v_s[m, :, :, head:] = jnp.ones(v_s.shape[1:3] + (head,), jnp.bfloat16)

    for copy in small:
        copy.wait()

    every = tiles * ring
    first_tile = me * tiles

    def fill_bias(t, carry):
        count = counts[t]
        places = []
        for j in range(lists.shape[1]):
            place = lists[t, j] - first_tile + RIM_T
            place = jnp.where(place < 0, place + every, place)
            place = jnp.where(place >= every, place - every, place)
            places.append(jnp.where(j < count, place, -1))
        for c in range(3 * tiles):
            if c < tiles:
                want = RIM_T + c
            elif c < 2 * tiles:
                want = jnp.where(parity == 0, RIM_T + tiles + c - tiles, RIM_T - tiles + c - tiles)
            else:
                want = jnp.where(parity == 0, RIM_T - tiles + c - 2 * tiles, RIM_T + tiles + c - 2 * tiles)
            hit = places[0] == want
            for place in places[1:]:
                hit = jnp.logical_or(hit, place == want)
            bias[t, c] = jnp.where(hit, 0.0, MASKED)
        return carry

    lax.fori_loop(0, tiles, fill_bias, 0)

    query_scale = math.log2(math.e) / math.sqrt(head)
    x_local.wait()

    def norm_own(m):
        xn[m] = norm_rows(xs[0, m], gain1[...].reshape(1, width))

    def project_own(h):
        both = xn[...].reshape(members * rows, width)
        made = dot(both, wproj[h])
        for m in range(members):
            here = slice(m * rows, (m + 1) * rows)
            q_s[m, h] = (made[here, :head] * query_scale).astype(jnp.bfloat16)
            k_s[m, h, :rows] = made[here, head:2 * head].astype(jnp.bfloat16)
            v_s[m, h, :rows, :head] = made[here, 2 * head:].astype(jnp.bfloat16)

    def project_rim(m, lo, hi):
        while lo < hi:
            slot, at = ORDER[m][lo]
            end = lo + 1
            while end < hi and ORDER[m][end] == (slot, at + end - lo):
                end += 1
            place = slice(lo * tile, end * tile)
            normed = norm_rows(xs[slot, m, at * tile:(at + end - lo) * tile],
                               gain1[...].reshape(1, width))
            for h in range(HEADS):
                made = dot(normed, wproj[h, :, head:]).astype(jnp.bfloat16)
                k_s[m, h, place] = made[:, :head]
                v_s[m, h, place, :head] = made[:, head:]
            lo = end

    def score(m, h, lo, hi):
        return lax.dot_general(
            q_s[m, h], k_s[m, h, lo * tile:hi * tile], (((1,), (1,)), ((), ())),
            preferred_element_type=jnp.float32)

    def weigh(m, h, lo, hi, last, scores):
        marks = [[bias[t, ORDER[m][c][0] * tiles + ORDER[m][c][1]] for c in range(lo, hi)]
                 for t in range(tiles)]
        packed, fades = [], []
        for t in range(tiles):
            here = slice(t * tile, (t + 1) * tile)
            parts = [scores[here, c * tile:(c + 1) * tile] + marks[t][c] for c in range(hi - lo)]
            best = parts[0]
            for p in parts[1:]:
                best = jnp.maximum(best, p)
            best = jnp.broadcast_to(jnp.max(best, axis=-1, keepdims=True), (tile, tile))
            if lo > 0:
                old = top[m, h, here, :]
                best = jnp.maximum(best, old)
                fades.append(jnp.exp2(old - best))
            if not last:
                top[m, h, here, :] = best
            packed.append(jnp.concatenate(
                [jnp.exp2(p - best).astype(jnp.bfloat16) for p in parts], axis=1))
        blended = dot(jnp.concatenate(packed, axis=0), v_s[m, h, lo * tile:hi * tile])
        if lo > 0:
            fade = jnp.concatenate(fades, axis=0)
            blended = blended + acc[m, h] * jnp.concatenate([fade, fade], axis=1)
        if last:
            att[m, h] = (blended[:, :head] / blended[:, head:]).astype(jnp.bfloat16)
        else:
            acc[m, h] = blended

    def attend(pairs, lo, hi, last=False):
        ahead = score(*pairs[0], lo, hi)
        for i, (m, h) in enumerate(pairs):
            scores = ahead
            if i + 1 < len(pairs):
                ahead = score(*pairs[i + 1], lo, hi)
            weigh(m, h, lo, hi, last, scores)

    def heads_of(m):
        return [(m, h) for h in range(HEADS)]

    def mix(m):
        blended = jnp.concatenate([att[m, h] for h in range(HEADS)], axis=1)
        middle = (xs[0, m].astype(jnp.float32) + dot(blended, wo[...])).astype(jnp.bfloat16)
        mid[m] = middle
        nrm[m] = norm_rows(middle, gain2[...].reshape(1, width))

    def expand(m):
        for c in range(inner // CUT):
            cut = slice(c * CUT, (c + 1) * CUT)
            hid[m, :, cut] = gelu(dot(nrm[m], up[:, cut])).astype(jnp.bfloat16)

    def finish(m):
        out_ref[m] = (mid[m].astype(jnp.float32) + dot(hid[m], down[...])).astype(jnp.bfloat16)

    def relay(first, last):
        for i in range(first, last):
            to_partner[i].wait_recv()
            to_onward[i].start()

    def far(first, last):
        for i in range(first, last):
            to_onward[i].wait_recv()

    def have_local(copies):
        for copy in copies:
            copy.wait()

    def near(units):
        for unit in units:
            unit.pass_near()

    def far_weights(units):
        for unit in units:
            unit.pass_far()

    def have(units):
        for unit in units:
            unit.have()


    norm_own(0)
    norm_own(1)
    relay(0, 1)
    near(proj_units[0:1])
    have_local(proj_local[0])
    relay(1, 2)
    have(proj_units[0:1])
    for h in range(HEADS):
        project_own(h)
        relay(h + 2, h + 3)
        if h + 1 < HEADS:
            near(proj_units[h + 1:h + 2])
        attend([(m, h) for m in range(members)], 0, tiles)
        if h + 1 < HEADS:
            have_local(proj_local[h + 1])
            far_weights(proj_units[h + 1:h + 2])
            have(proj_units[h + 1:h + 2])
    relay(6, 8)
    near(wo_units)
    far(0, 4)
    project_rim(0, tiles, tiles + 6)
    relay(8, 9)
    attend(heads_of(0), tiles, tiles + 6)
    relay(9, 11)
    far(4, 8)
    project_rim(0, tiles + 6, 3 * tiles)
    relay(11, 12)
    attend(heads_of(0), tiles + 6, 3 * tiles, True)
    near(up_units[:UP_CUTS // 2])
    have_local([rest_local["wo"]])
    have(wo_units)
    relay(12, 13)
    mix(0)
    relay(13, 14)
    project_rim(1, tiles, tiles + 3)
    attend(heads_of(1), tiles, tiles + 3)
    relay(14, 16)
    far(8, 12)
    project_rim(1, tiles + 3, tiles + 6)
    attend(heads_of(1), tiles + 3, tiles + 6)
    near(up_units[UP_CUTS // 2:])
    near(down_shared)
    have_local([rest_local["up"]])
    have(up_units)
    expand(0)
    far(12, 16)
    project_rim(1, tiles + 6, 3 * tiles)
    attend(heads_of(1), tiles + 6, 3 * tiles, True)
    mix(1)
    far_weights(down_shared)
    near(down_direct)
    expand(1)
    have_local([rest_local["down"]])
    have(down_units)
    for m in range(members):
        finish(m)

    for sem in (xp_send, xf_send):
        pltpu.make_async_remote_copy(
            src_ref=xs.at[1], dst_ref=xs.at[2], send_sem=sem, recv_sem=w_recv.at[0],
            device_id={"mesh": partner}, device_id_type=MESH).wait_send()
    for way, size in enumerate(moved):
        if size:
            whole = down.at[pl.ds(0, size)]
            pltpu.make_async_remote_copy(
                src_ref=whole, dst_ref=whole, send_sem=w_send.at[way], recv_sem=w_recv.at[0],
                device_id={"member": twin}, device_id_type=MESH).wait_send()


def solution(mesh):
    ring, party = mesh.shape["mesh"], mesh.shape["member"]

    def on_device(node_states, projection, output_weight, up_weight, down_weight,
                  attention_gain, feedforward_gain, tile_lists, tile_counts):
        members, rows, width = node_states.shape
        tiles = tile_lists.shape[0]
        head = width // HEADS
        inner = up_weight.shape[1]
        hbm = pl.BlockSpec(memory_space=pltpu.HBM)
        bf16, f32 = jnp.bfloat16, jnp.float32
        copies = members * tiles * PIECES
        keys = 3 * rows
        return pl.pallas_call(
            functools.partial(kernel, ring, party, tiles),
            out_shape=pltpu.VMEM(node_states.shape, bf16),
            in_specs=[hbm] * 9,
            out_specs=pl.BlockSpec(memory_space=pltpu.VMEM),
            scratch_shapes=[
                pltpu.VMEM((3, members, rows, width), bf16),
                pltpu.VMEM((members, rows, width), bf16),
                pltpu.VMEM((HEADS, width, 3 * head), bf16),
                pltpu.VMEM((width, width), bf16),
                pltpu.VMEM((width, inner), bf16),
                pltpu.VMEM((inner, width), bf16),
                pltpu.VMEM((members, HEADS, rows, head), bf16),
                pltpu.VMEM((members, HEADS, keys, head), bf16),
                pltpu.VMEM((members, HEADS, keys, 2 * head), bf16),
                pltpu.VMEM((members, HEADS, rows, 2 * head), f32),
                pltpu.VMEM((members, HEADS, rows, head), f32),
                pltpu.VMEM((members, HEADS, rows, head), bf16),
                pltpu.VMEM((members, rows, inner), bf16),
                pltpu.VMEM((members, rows, width), bf16),
                pltpu.VMEM((members, rows, width), bf16),
                pltpu.SMEM((tiles, 3 * tiles), f32),
                pltpu.VMEM((width,), f32),
                pltpu.VMEM((width,), f32),
                pltpu.SMEM(tile_lists.shape, jnp.int32),
                pltpu.SMEM(tile_counts.shape, jnp.int32),
                pltpu.SemaphoreType.DMA((8 + HEADS,)),
                pltpu.SemaphoreType.DMA,
                pltpu.SemaphoreType.DMA((copies,)),
                pltpu.SemaphoreType.DMA,
                pltpu.SemaphoreType.DMA((copies,)),
                pltpu.SemaphoreType.DMA((5,)),
                pltpu.SemaphoreType.DMA((SLOTS,)),
            ],
            compiler_params=pltpu.CompilerParams(
                collective_id=0, has_side_effects=True, vmem_limit_bytes=60000000
            ),
        )(node_states, projection, output_weight, up_weight, down_weight,
          attention_gain, feedforward_gain, tile_lists, tile_counts)

    in_specs = (
        P("member", "mesh", None), P("member", None), P("member", None),
        P("member", None), P("member", None), P(), P(), P("mesh", None), P("mesh"),
    )
    return jax.shard_map(
        on_device, mesh=mesh, in_specs=in_specs,
        out_specs=P("member", "mesh", None), check_vma=False)
```

time: 51.5 us -> 45.4 us (0.88)
  Pallas kernels: 50.4 us -> 44.2 us
    pallas_call x1, Pallas kernels: 50.4 us -> 44.2 us  [on_device(): pl.pallas_call(functools.partial(kernel, ring, party, tiles), out_shape=p...]
where the time goes in v2:
time: 45.4 us; the launch traced here: 45.2 us
  Pallas kernels  44.2 us (97%)
  local copies, waits for them, and re-layouts  0.97 us (2%)
    pallas_call x1, Pallas kernels, on_device(): pl.pallas_call(functools.partial(kernel, ring, party, tiles), out_shape=p...  44.2 us
    unnamed x1, local copies, waits for them, and re-layouts  0.97 us

profile of v2, /device:TPU:0, one launch (start us, length us, event | category | flops | bytes accessed | tf_op | source)
XLA Modules:
  0.0 45.2 jit_solution(10696680097793963814)
XLA Ops:
  0.0 44.2 %shard_map.91 = bf16[2,512,512]{2,1,0:T(8,128)(2,1)S(1)} custom-call(bf16[2,512,512]{2,1,0:T(8,128)(2,1)} %x_hbm.1, bf16[128,1536]{1,0:T(8,128)(2,1)} %proj_hbm.1, bf16[128,512]{1,0:T(8,128)(2,1)} %wo_hbm.1, bf16[128,2048]{1,0:T(8,128)(2,1)} %up_hbm.1, bf16[512,512]{1,0:T(8,128)(2,1)} %down_hbm.1, f32[512]{0:T(512)} %gain1_hbm.1, f32[512]{0:T(512)} %gain2_hbm.1, ...), custom_call_target="tpu_custom_call" | custom-call | tf_op jit(solution)/shard_map/pallas_call | solution.py:465
  44.2 1.0 %copy.11 = bf16[2,512,512]{2,1,0:T(8,128)(2,1)} copy(bf16[2,512,512]{2,1,0:T(8,128)(2,1)S(1)} %shard_map.91) | data formatting | bytes 2097152

commit v3 on v2

--- a/solution.py
+++ b/solution.py
@@ -13,13 +13,16 @@
 MESH = pl.DeviceIdType.MESH
 MASKED = -1e30
 EPS = 1e-05
-SLOTS = 42
+SLOTS = 24
 PROJ_VIA = (None, None, None, None)
-UP_CUTS = 2
-DOWN_SHARED = 12
-DOWN_CUTS = 3
+UP_CUTS = 4
+DOWN_SHARED = 10
+DOWN_CUTS = 2
 PIECES = 2
 CUT = 256
+MIX_CUTS = 1
+LAST = 2
+FAR = [4, 8, 10, 12, 14, 17]
 ORDER = [[(0, 0), (0, 1), (0, 2), (0, 3), (1, 0), (1, 1), (1, 2), (1, 3), (2, 0), (2, 1), (2, 2), (2, 3)], [(0, 0), (0, 1), (0, 2), (0, 3), (1, 0), (1, 1), (1, 2), (2, 0), (2, 1), (1, 3), (2, 2), (2, 3)]]
 
 
@@ -30,9 +33,10 @@
     return (center * lax.rsqrt(spread + EPS) * gain).astype(jnp.bfloat16)
 
 
-def gelu(value):
-    inner = math.sqrt(2.0 / math.pi) * (value + 0.044715 * value * value * value)
-    return 0.5 * value * (1.0 + jnp.tanh(inner))
+def twice_gelu(value):
+    scale = math.sqrt(2.0 / math.pi)
+    inner = value * (value * value * (0.044715 * scale) + scale)
+    return (value * jnp.tanh(inner) + value).astype(jnp.bfloat16)
 
 
 def dot(a, b):
@@ -43,7 +47,7 @@
     ring, party, tiles,
     x_hbm, proj_hbm, wo_hbm, up_hbm, down_hbm, gain1_hbm, gain2_hbm, lists_hbm, counts_hbm,
     out_ref,
-    xs, xn, wproj, wo, up, down, q_s, k_s, v_s, acc, top, att, hid, mid, nrm, bias,
+    xs, xn, wproj, wo, up, down, q_s, k_s, v_s, acc, top, att, hid, mid, nrm, part_s, bias,
     gain1, gain2, lists, counts,
     local_sem, xp_send, xp_recv, xf_send, xf_recv, w_send, w_recv,
 ):
@@ -63,8 +67,6 @@
     twin = mine + 1 - 2 * core
     across = [lax.rem(mine + 2 * d, party) for d in range(1, groups)]
 
-    w_local = []
-
     def part(ref, who, depth, start, size):
         return ref.at[pl.ds(pl.multiple_of(who * depth + start, 16), size)]
 
@@ -81,14 +83,6 @@
     for peer in [twin] + across:
         pl.semaphore_signal(barrier, inc=1, device_id={"member": peer}, device_id_type=MESH)
 
-    local_count = [5]
-
-    def local(src, dst):
-        copy = pltpu.make_async_copy(src, dst, local_sem.at[local_count[0]])
-        local_count[0] += 1
-        copy.start()
-        return copy
-
     def head_blocks(h, who, start, size):
         depth = proj_hbm.shape[0]
         return [(proj_hbm.at[pl.ds(start, size), pl.ds(j * width + h * head, head)],
@@ -108,26 +102,31 @@
     proj_local = []
     for h in range(HEADS):
         for s, d in head_blocks(h, mine, 0, proj_hbm.shape[0]):
-            pltpu.make_async_copy(s, d, local_sem.at[8 + h]).start()
-        whole = wproj.at[h, pl.ds(0, proj_hbm.shape[0])]
-        proj_local.append([pltpu.make_async_copy(whole, whole, local_sem.at[8 + h])])
-    rest_local = {name: local(shard, part(whole, mine, shard.shape[0], 0, shard.shape[0]))
-                  for name, shard, whole in
-                  (("wo", wo_hbm, wo), ("up", up_hbm, up), ("down", down_hbm, down))}
-
-    used = [0]
+            pltpu.make_async_copy(s, d, local_sem.at[6]).start()
+    whole = down.at[pl.ds(0, 3 * proj_hbm.shape[0])]
+    proj_local.append([pltpu.make_async_copy(whole, whole, local_sem.at[6])])
+    rest_rows = 0
+    for shard, whole in ((wo_hbm, wo), (up_hbm, up), (down_hbm, down)):
+        pltpu.make_async_copy(
+            shard, part(whole, mine, shard.shape[0], 0, shard.shape[0]), local_sem.at[5]).start()
+        rest_rows += math.prod(shard.shape) // width
+    whole = down.at[pl.ds(0, rest_rows)]
+    rest_local = pltpu.make_async_copy(whole, whole, local_sem.at[5])
+
+    groups_of = {}
     moved = [0] * 5
 
     odd = lax.rem(me // 2, 2)
     beside = me + 2 - 4 * odd
 
     class Stream:
-        def __init__(self, way, pairs, target):
+        def __init__(self, way, pairs, target, group=None):
             self.pairs, self.way = pairs, way
-            self.index = used[0]
-            used[0] += 1
-            self.size = sum(math.prod(s.shape) for s, _ in pairs) // width
-            moved[way] += self.size
+            self.group = groups_of.setdefault(group or len(groups_of), [len(groups_of), 0, False])
+            self.index = self.group[0]
+            size = sum(math.prod(s.shape) for s, _ in pairs) // width
+            self.group[1] += size
+            moved[way] += size
             self.target = target
 
         def copy(self, src, dst):
@@ -140,13 +139,18 @@
                 self.copy(s, d).start()
 
         def wait_recv(self):
-            whole = down.at[pl.ds(0, self.size)]
-            self.copy(whole, whole).wait_recv()
+            if not self.group[2]:
+                self.group[2] = True
+                whole = down.at[pl.ds(0, self.group[1])]
+                self.copy(whole, whole).wait_recv()
 
     class Unit:
         def __init__(self, name, start, size, via=None):
             over_pairs, near_pairs, mate_pairs, far_pairs = [], [], [], []
-            self.twin = [Stream(0, blocks_of(name, mine, start, size), {"member": twin})]
+            kind = name[0]
+            self.twin = [Stream(0, blocks_of(name, mine, start, size), {"member": twin},
+                                "own" if kind == "proj" else "own rest")]
+            passed = None if kind == "proj" else "passed " + kind
             self.over, self.near, self.mate, self.far = [], [], [], []
             for d in range(1, groups):
                 giver = lax.rem(mine + party - 2 * d, party)
@@ -160,12 +164,12 @@
                 self.over.append(Stream(1, blocks_of(name, mine, got, part_size),
                                         {"member": across[d - 1]}))
                 here = [(t, t) for _, t in blocks_of(name, giver, got, part_size)]
-                self.near.append(Stream(2, here, {"member": twin}))
+                self.near.append(Stream(2, here, {"member": twin}, passed))
                 if via is not None:
                     self.mate.append(Stream(3, here, {"mesh": mate}))
                     self.far.append(Stream(
                         4, [(t, t) for _, t in blocks_of(name, giver, other, part_size)],
-                        {"member": twin}))
+                        {"member": twin}, passed))
 
         def send_twin(self):
             for stream in self.twin:
@@ -207,16 +211,18 @@
     all_units = proj_units + wo_units + up_units + down_units
 
     piece = tile // PIECES
-    steps = [(m, i * piece) for m in range(members) for i in range(rows // piece)]
+    steps = [(m, i * piece, piece) for m in range(members) for i in range(rows // piece)]
+    m, start, size = steps.pop()
+    steps += [(m, start + i * (size // LAST), size // LAST) for i in range(LAST)]
     to_partner, to_onward = [], []
-    for i, (m, start) in enumerate(steps):
+    for i, (m, start, size) in enumerate(steps):
         to_partner.append(pltpu.make_async_remote_copy(
-            src_ref=x_hbm.at[m, pl.ds(start, piece)], dst_ref=xs.at[1, m, pl.ds(start, piece)],
+            src_ref=x_hbm.at[m, pl.ds(start, size)], dst_ref=xs.at[1, m, pl.ds(start, size)],
             send_sem=xp_send, recv_sem=xp_recv.at[i],
             device_id={"mesh": partner}, device_id_type=MESH))
         to_onward.append(pltpu.make_async_remote_copy(
-            src_ref=xs.at[1, m, pl.ds(start, piece)], dst_ref=xs.at[2, m, pl.ds(start, piece)],
-            send_sem=xf_send, recv_sem=xf_recv.at[i],
+            src_ref=xs.at[1, m, pl.ds(start, size)], dst_ref=xs.at[2, m, pl.ds(start, size)],
+            send_sem=xf_send, recv_sem=xf_recv.at[FAR.index(next(f for f in FAR if i < f))],
             device_id={"mesh": onward}, device_id_type=MESH))
 
     pl.semaphore_wait(barrier, 4 + len(across))
@@ -296,18 +302,20 @@
                 v_s[m, h, place, :head] = made[:, head:]
             lo = end
 
-    def score(m, h, lo, hi):
+    everyone = (0, tiles)
+
+    def score(m, h, lo, hi, who):
         return lax.dot_general(
-            q_s[m, h], k_s[m, h, lo * tile:hi * tile], (((1,), (1,)), ((), ())),
-            preferred_element_type=jnp.float32)
-
-    def weigh(m, h, lo, hi, last, scores):
-        marks = [[bias[t, ORDER[m][c][0] * tiles + ORDER[m][c][1]] for c in range(lo, hi)]
-                 for t in range(tiles)]
+            q_s[m, h, who[0] * tile:who[1] * tile], k_s[m, h, lo * tile:hi * tile],
+            (((1,), (1,)), ((), ())), preferred_element_type=jnp.float32)
+
+    def weigh(m, h, lo, hi, last, scores, who):
         packed, fades = [], []
-        for t in range(tiles):
+        for t in range(who[0], who[1]):
             here = slice(t * tile, (t + 1) * tile)
-            parts = [scores[here, c * tile:(c + 1) * tile] + marks[t][c] for c in range(hi - lo)]
+            mine_rows = slice((t - who[0]) * tile, (t - who[0] + 1) * tile)
+            parts = [scores[mine_rows, (c - lo) * tile:(c - lo + 1) * tile]
+                     + bias[t, ORDER[m][c][0] * tiles + ORDER[m][c][1]] for c in range(lo, hi)]
             best = parts[0]
             for p in parts[1:]:
                 best = jnp.maximum(best, p)
@@ -320,48 +328,100 @@
                 top[m, h, here, :] = best
             packed.append(jnp.concatenate(
                 [jnp.exp2(p - best).astype(jnp.bfloat16) for p in parts], axis=1))
+        rows_here = slice(who[0] * tile, who[1] * tile)
         blended = dot(jnp.concatenate(packed, axis=0), v_s[m, h, lo * tile:hi * tile])
         if lo > 0:
             fade = jnp.concatenate(fades, axis=0)
-            blended = blended + acc[m, h] * jnp.concatenate([fade, fade], axis=1)
+            blended = blended + acc[m, h, rows_here] * jnp.concatenate([fade, fade], axis=1)
         if last:
-            att[m, h] = (blended[:, :head] / blended[:, head:]).astype(jnp.bfloat16)
+            att[m, h, rows_here] = (blended[:, :head] / blended[:, head:]).astype(jnp.bfloat16)
         else:
-            acc[m, h] = blended
-
-    def attend(pairs, lo, hi, last=False):
-        ahead = score(*pairs[0], lo, hi)
-        for i, (m, h) in enumerate(pairs):
-            scores = ahead
+            acc[m, h, rows_here] = blended
+
+    def attend_steps(pairs, lo, hi, last=False, who=everyone):
+        ahead = [score(*pairs[0], lo, hi, who)]
+
+        def step(i):
+            scores = ahead.pop()
             if i + 1 < len(pairs):
-                ahead = score(*pairs[i + 1], lo, hi)
-            weigh(m, h, lo, hi, last, scores)
+                ahead.append(score(*pairs[i + 1], lo, hi, who))
+            weigh(*pairs[i], lo, hi, last, scores, who)
+
+        return [functools.partial(step, i) for i in range(len(pairs))]
+
+    def run(*lists):
+        order = sorted(((i + 0.5) / len(steps), n, i)
+                       for n, steps in enumerate(lists) for i in range(len(steps)))
+        for _, n, i in order:
+            lists[n][i]()
+
+    def attend(pairs, lo, hi, last=False, who=everyone):
+        run(attend_steps(pairs, lo, hi, last, who))
 
     def heads_of(m):
         return [(m, h) for h in range(HEADS)]
 
-    def mix(m):
-        blended = jnp.concatenate([att[m, h] for h in range(HEADS)], axis=1)
-        middle = (xs[0, m].astype(jnp.float32) + dot(blended, wo[...])).astype(jnp.bfloat16)
-        mid[m] = middle
-        nrm[m] = norm_rows(middle, gain2[...].reshape(1, width))
+    def mix(m, who=everyone):
+        split = (who[1] - who[0]) * tile // MIX_CUTS
+        spans = [slice(who[0] * tile + i * split, who[0] * tile + (i + 1) * split)
+                 for i in range(MIX_CUTS)]
+        mixed = [dot(jnp.concatenate([att[m, h, span] for h in range(HEADS)], axis=1), wo[...])
+                 for span in spans]
+        for span, value in zip(spans, mixed):
+            middle = (xs[0, m, span].astype(jnp.float32) + value).astype(jnp.bfloat16)
+            mid[m, span] = middle
+            nrm[m, span] = norm_rows(middle, gain2[...].reshape(1, width))
+
+    def expand_steps(m, who=everyone):
+        rows_here = slice(who[0] * tile, who[1] * tile)
+
+        def step(c):
+            span = slice(c * CUT, (c + 1) * CUT)
+            hid[m, rows_here, span] = twice_gelu(dot(nrm[m, rows_here], up[:, span]))
+
+        return [functools.partial(step, c) for c in range(inner // CUT)]
 
     def expand(m):
-        for c in range(inner // CUT):
-            cut = slice(c * CUT, (c + 1) * CUT)
-            hid[m, :, cut] = gelu(dot(nrm[m], up[:, cut])).astype(jnp.bfloat16)
-
-    def finish(m):
-        out_ref[m] = (mid[m].astype(jnp.float32) + dot(hid[m], down[...])).astype(jnp.bfloat16)
+        run(expand_steps(m))
+
+    two = 2 * down_hbm.shape[0]
+    chip = mine - core
+    own_rows = pl.ds(pl.multiple_of(chip * down_hbm.shape[0], 128), two)
+    far_rows = [pl.ds(pl.multiple_of(lax.rem(chip + 2 * d, party) * down_hbm.shape[0], 128), two)
+                for d in range(1, groups)]
+
+    def begin_steps(m, who=everyone):
+        rows_here = slice(who[0] * tile, who[1] * tile)
+
+        def step(c):
+            span = slice(c * 256, (c + 1) * 256)
+            part_s[m, rows_here, span] = (2.0 * mid[m, rows_here, span].astype(jnp.float32)
+                                          + dot(hid[m, rows_here, own_rows], down[own_rows, span]))
+
+        return [functools.partial(step, c) for c in range(width // 256)]
+
+    def end_steps(m):
+        def step(c):
+            span = slice(c * 256, (c + 1) * 256)
+            total = part_s[m, :, span]
+            for there in far_rows:
+                total = total + dot(hid[m, :, there], down[there, span])
+            out_ref[m, :, span] = (0.5 * total).astype(jnp.bfloat16)
+
+        return [functools.partial(step, c) for c in range(width // 256)]
 
     def relay(first, last):
         for i in range(first, last):
             to_partner[i].wait_recv()
             to_onward[i].start()
 
-    def far(first, last):
-        for i in range(first, last):
-            to_onward[i].wait_recv()
+    def far(last):
+        n = FAR.index(last)
+        rows_in = sum(size for _, _, size in steps[FAR[n - 1] if n else 0:last])
+        whole = down.at[pl.ds(0, rows_in)]
+        pltpu.make_async_remote_copy(
+            src_ref=whole, dst_ref=whole, send_sem=xf_send, recv_sem=xf_recv.at[n],
+            device_id={"mesh": onward}, device_id_type=MESH).wait_recv()
 
     def have_local(copies):
         for copy in copies:
@@ -389,53 +449,77 @@
     have(proj_units[0:1])
     for h in range(HEADS):
         project_own(h)
-        relay(h + 2, h + 3)
         if h + 1 < HEADS:
+            if h == 1:
+                relay(3, 4)
             near(proj_units[h + 1:h + 2])
+            if h == 0:
+                relay(2, 3)
+            if h == 2:
+                relay(5, 6)
+        if h == 3:
+            relay(6, 7)
         attend([(m, h) for m in range(members)], 0, tiles)
         if h + 1 < HEADS:
-            have_local(proj_local[h + 1])
-            far_weights(proj_units[h + 1:h + 2])
+            if h == 1:
+                relay(4, 5)
             have(proj_units[h + 1:h + 2])
-    relay(6, 8)
+    relay(7, 8)
     near(wo_units)
-    far(0, 4)
+    far(4)
     project_rim(0, tiles, tiles + 6)
     relay(8, 9)
     attend(heads_of(0), tiles, tiles + 6)
-    relay(9, 11)
-    far(4, 8)
+    relay(9, 10)
+    project_rim(1, tiles, tiles + 1)
+    have_local([rest_local])
+    have(wo_units)
+    relay(10, 11)
+    far(8)
     project_rim(0, tiles + 6, 3 * tiles)
     relay(11, 12)
+    near(up_units[:1])
     attend(heads_of(0), tiles + 6, 3 * tiles, True)
-    near(up_units[:UP_CUTS // 2])
-    have_local([rest_local["wo"]])
-    have(wo_units)
+    project_rim(1, tiles + 1, tiles + 2)
+    mix(0)
     relay(12, 13)
-    mix(0)
+    near(up_units[1:2])
+    attend(heads_of(1), tiles, tiles + 2)
     relay(13, 14)
-    project_rim(1, tiles, tiles + 3)
-    attend(heads_of(1), tiles, tiles + 3)
-    relay(14, 16)
-    far(8, 12)
-    project_rim(1, tiles + 3, tiles + 6)
-    attend(heads_of(1), tiles + 3, tiles + 6)
-    near(up_units[UP_CUTS // 2:])
-    near(down_shared)
-    have_local([rest_local["up"]])
+    far(10)
+    project_rim(1, tiles + 2, tiles + 4)
+    near(up_units[2:3])
+    attend(heads_of(1), tiles + 2, tiles + 4)
+    relay(14, 15)
+    near(up_units[3:])
+    relay(15, 15 + LAST)
+    far(12)
+    project_rim(1, tiles + 4, tiles + 6)
+    attend(heads_of(1), tiles + 4, tiles + 6)
     have(up_units)
+    near(down_shared[:1])
     expand(0)
-    far(12, 16)
-    project_rim(1, tiles + 6, 3 * tiles)
-    attend(heads_of(1), tiles + 6, 3 * tiles, True)
-    mix(1)
-    far_weights(down_shared)
-    near(down_direct)
-    expand(1)
-    have_local([rest_local["down"]])
+    near(down_shared[1:])
+    run(begin_steps(0))
+    far(14)
+    project_rim(1, tiles + 6, tiles + 7)
+    far(15 + LAST)
+    project_rim(1, tiles + 7, 3 * tiles)
+    half = tiles // 2
+    first, second = (0, half), (half, tiles)
+    attend(heads_of(1), tiles + 6, 3 * tiles, True, first)
+    far_weights(down_shared[:1])
+    near(down_direct[:1])
+    mix(1, first)
+    run(attend_steps(heads_of(1), tiles + 6, 3 * tiles, True, second), expand_steps(1, first)[:4])
+    far_weights(down_shared[1:])
+    near(down_direct[1:])
+    mix(1, second)
+    run(expand_steps(1, first)[4:], expand_steps(1, second)[:4])
+    run(begin_steps(1, first), expand_steps(1, second)[4:])
+    run(begin_steps(1, second))
     have(down_units)
-    for m in range(members):
-        finish(m)
+    run(end_steps(0), end_steps(1))
 
     for sem in (xp_send, xf_send):
         pltpu.make_async_remote_copy(
@@ -460,7 +544,7 @@
         inner = up_weight.shape[1]
         hbm = pl.BlockSpec(memory_space=pltpu.HBM)
         bf16, f32 = jnp.bfloat16, jnp.float32
-        copies = members * tiles * PIECES
+        copies = members * tiles * PIECES + LAST - 1
         keys = 3 * rows
         return pl.pallas_call(
             functools.partial(kernel, ring, party, tiles),
@@ -483,16 +567,17 @@
                 pltpu.VMEM((members, rows, inner), bf16),
                 pltpu.VMEM((members, rows, width), bf16),
                 pltpu.VMEM((members, rows, width), bf16),
+                pltpu.VMEM((members, rows, width), f32),
                 pltpu.SMEM((tiles, 3 * tiles), f32),
                 pltpu.VMEM((width,), f32),
                 pltpu.VMEM((width,), f32),
                 pltpu.SMEM(tile_lists.shape, jnp.int32),
                 pltpu.SMEM(tile_counts.shape, jnp.int32),
-                pltpu.SemaphoreType.DMA((8 + HEADS,)),
+                pltpu.SemaphoreType.DMA((7,)),
                 pltpu.SemaphoreType.DMA,
                 pltpu.SemaphoreType.DMA((copies,)),
                 pltpu.SemaphoreType.DMA,
-                pltpu.SemaphoreType.DMA((copies,)),
+                pltpu.SemaphoreType.DMA((len(FAR),)),
                 pltpu.SemaphoreType.DMA((5,)),
                 pltpu.SemaphoreType.DMA((SLOTS,)),
             ],

time: 45.4 us -> 43.3 us (0.954)
  Pallas kernels: 44.2 us -> 42.2 us
    pallas_call x1, Pallas kernels: 44.2 us -> 42.2 us  [on_device(): pl.pallas_call(functools.partial(kernel, ring, party, tiles), out_shape=p...]
where the time goes in v3:
time: 43.3 us; the launch traced here: 43.2 us
  Pallas kernels  42.2 us (97%)
  local copies, waits for them, and re-layouts  0.97 us (2%)
    pallas_call x1, Pallas kernels, on_device(): pl.pallas_call(functools.partial(kernel, ring, party, tiles), out_shape=p...  42.2 us
    unnamed x1, local copies, waits for them, and re-layouts  0.97 us

profile of v3, /device:TPU:0, one launch (start us, length us, event | category | flops | bytes accessed | tf_op | source)
XLA Modules:
  0.0 43.2 jit_solution(14507827562460415297)
XLA Ops:
  0.0 42.2 %shard_map.91 = bf16[2,512,512]{2,1,0:T(8,128)(2,1)S(1)} custom-call(bf16[2,512,512]{2,1,0:T(8,128)(2,1)} %x_hbm.1, bf16[128,1536]{1,0:T(8,128)(2,1)} %proj_hbm.1, bf16[128,512]{1,0:T(8,128)(2,1)} %wo_hbm.1, bf16[128,2048]{1,0:T(8,128)(2,1)} %up_hbm.1, bf16[512,512]{1,0:T(8,128)(2,1)} %down_hbm.1, f32[512]{0:T(512)} %gain1_hbm.1, f32[512]{0:T(512)} %gain2_hbm.1, ...), custom_call_target="tpu_custom_call" | custom-call | tf_op jit(solution)/shard_map/pallas_call | solution.py:549
  42.2 1.0 %copy.11 = bf16[2,512,512]{2,1,0:T(8,128)(2,1)} copy(bf16[2,512,512]{2,1,0:T(8,128)(2,1)S(1)} %shard_map.91) | data formatting | bytes 2097152

commit v4 on v3

--- a/solution.py
+++ b/solution.py
@@ -491,10 +491,10 @@
     near(up_units[2:3])
     attend(heads_of(1), tiles + 2, tiles + 4)
     relay(14, 15)
-    near(up_units[3:])
     relay(15, 15 + LAST)
     far(12)
     project_rim(1, tiles + 4, tiles + 6)
+    near(up_units[3:])
     attend(heads_of(1), tiles + 4, tiles + 6)
     have(up_units)
     near(down_shared[:1])

time: 43.3 us -> 43.3 us (level)
  no operation moved by 1% of the time
where the time goes in v4:
time: 43.3 us; the launch traced here: 43.2 us
  Pallas kernels  42.2 us (97%)
  local copies, waits for them, and re-layouts  0.97 us (2%)
    pallas_call x1, Pallas kernels, on_device(): pl.pallas_call(functools.partial(kernel, ring, party, tiles), out_shape=p...  42.2 us
    unnamed x1, local copies, waits for them, and re-layouts  0.97 us

profile of v4, /device:TPU:0, one launch (start us, length us, event | category | flops | bytes accessed | tf_op | source)
XLA Modules:
  0.0 43.2 jit_solution(15354903373416795876)
XLA Ops:
  0.0 42.2 %shard_map.91 = bf16[2,512,512]{2,1,0:T(8,128)(2,1)S(1)} custom-call(bf16[2,512,512]{2,1,0:T(8,128)(2,1)} %x_hbm.1, bf16[128,1536]{1,0:T(8,128)(2,1)} %proj_hbm.1, bf16[128,512]{1,0:T(8,128)(2,1)} %wo_hbm.1, bf16[128,2048]{1,0:T(8,128)(2,1)} %up_hbm.1, bf16[512,512]{1,0:T(8,128)(2,1)} %down_hbm.1, f32[512]{0:T(512)} %gain1_hbm.1, f32[512]{0:T(512)} %gain2_hbm.1, ...), custom_call_target="tpu_custom_call" | custom-call | tf_op jit(solution)/shard_map/pallas_call | solution.py:549
  42.2 1.0 %copy.11 = bf16[2,512,512]{2,1,0:T(8,128)(2,1)} copy(bf16[2,512,512]{2,1,0:T(8,128)(2,1)S(1)} %shard_map.91) | data formatting | bytes 2097152
